TPU v7x, 32 devices: a whole 2x2x4 slice. The times are simulated.
32 devices in a mesh: dom: 8 (over y, x, core), feat: 4 (over z).
Axes of the slice: x: 2, y: 2, z: 4, core: 2. Of those that a mesh axis runs over, the one named last changes fastest.
Arguments:
- features: bfloat16 [512, 65536], P('feat', 'dom'), may hold values from -3 to 3
- send_blocks: int32 [8, 8, 8], P('dom'), may hold values from 0 to 63, as said below
- counts: int32 [8, 8], P('dom'), may hold values from 0 to 8, as said below
- tile_blocks: int32 [24, 512], P(None, 'dom'), may hold values from 0 to 127, as said below
- neighbours: int32 [24, 65536], P(None, 'dom'), may hold values from 0 to 127
- degree: int32 [65536], P('dom'), may hold values from 1 to 24
- epsilon: float32 [1], replicated, may hold values from -0.3 to 0.6
- w_first: bfloat16 [512, 512], replicated, may hold values from -0.25 to 0.25
- b_first: float32 [512], replicated, may hold values from -3 to 3
- w_second: bfloat16 [512, 512], replicated, may hold values from -0.25 to 0.25
- b_second: float32 [512], replicated, may hold values from -3 to 3
Outputs:
- updated: bfloat16 [65536, 512], P(('dom', 'feat'))
Inputs may be any that keep to these rules, and one draw needn't show every extreme that they name: `send_blocks`: entry [q, p, s] is a row block of partition q; the entries of one pair (q, p) are distinct. counts[q, p] leading slots of send_blocks[q, p] are used; zero where q == p; in every draw some partition receives 8 blocks from every other partition. `tile_blocks`: an entry for a row block of partition p is below 64 (a row block of p) or equals 64 + q * 8 + s for a slot s of a partition q other than p.
All inputs are finite; a program needn't handle non-finite values.
Results may differ from a plain program's by a relative error of at most 0.0055.
Values may be sent and summed in bfloat16 or wider, within the bound.
A program may use at most 64 MiB of HBM per device.

v0:
```python
import jax
import jax.numpy as jnp
from jax import lax
from jax.sharding import PartitionSpec as P

BLOCK = 128


def over_tiles(table, tiles, offsets, weight):
    width, block_count = tiles.shape
    col_count = table.shape[1]
    block_size = table.shape[2]
    group = min(block_count, 16)
    steps = block_count // group
    tile_steps = tiles.reshape(width, steps, group).transpose(1, 0, 2)
    offset_steps = offsets.reshape(width, steps, group, block_size).transpose(1, 0, 2, 3)
    weight_steps = weight.reshape(width, steps, group, block_size).transpose(1, 0, 2, 3)
    source_ids = jnp.arange(block_size, dtype=jnp.int32)[:, None]

    def one_step(triple):
        gathered = table[triple[0]]
        onehot = jnp.where(
            triple[1][:, :, None, :] == source_ids,
            triple[2][:, :, None, :],
            jnp.zeros((), jnp.bfloat16),
        )
        return jnp.einsum("kgcs,kgsd->gcd", gathered, onehot, preferred_element_type=jnp.float32)

    result = lax.map(one_step, (tile_steps, offset_steps, weight_steps))
    return result.reshape(block_count, col_count, block_size)


def per_device(
    features,
    send_blocks,
    counts,
    tile_blocks,
    neighbours,
    degree,
    epsilon,
    w_first,
    b_first,
    w_second,
    b_second,
):
    col_count, row_count = features.shape
    part_count = lax.axis_size("dom")
    slot_count = send_blocks.shape[2]
    list_width = neighbours.shape[0]
    block_count = row_count // BLOCK
    feat_blocks = features.reshape(col_count, block_count, BLOCK).transpose(1, 0, 2)
    chosen = feat_blocks[send_blocks[0]]
    slot_used = jnp.arange(slot_count, dtype=jnp.int32)[None, :] < counts[0][:, None]
    chosen = jnp.where(slot_used[:, :, None, None], chosen, jnp.zeros_like(chosen))
    arrived = lax.all_to_all(chosen, "dom", split_axis=0, concat_axis=0, tiled=True).reshape(
        part_count * slot_count, col_count, BLOCK
    )
    live_mask = jnp.arange(list_width, dtype=jnp.int32)[:, None] < degree[None, :]
    halo_table = jnp.concatenate([feat_blocks, arrived], axis=0)
    near_blocks = over_tiles(halo_table, tile_blocks, neighbours, live_mask.astype(jnp.bfloat16))
    near_sum = near_blocks.transpose(1, 0, 2).reshape(col_count, row_count)
    mixed = ((1.0 + epsilon[0]) * features.astype(jnp.float32) + near_sum).astype(jnp.bfloat16)
    groups = lax.axis_size("feat")
    owned_rows = row_count // groups
    group_rows = min(owned_rows, 512)
    shaped = mixed.reshape(col_count, groups, owned_rows // group_rows, group_rows)
    parcel = lax.all_to_all(shaped, "feat", split_axis=1, concat_axis=0, tiled=True)
    flat_cols = parcel.reshape(parcel.shape[0], -1)
    pre_act = (
        lax.dot_general(
            flat_cols, w_first, (((0,), (0,)), ((), ())), preferred_element_type=jnp.float32
        )
        + b_first
    )
    activated = jax.nn.relu(pre_act).astype(jnp.bfloat16)
    return (jnp.dot(activated, w_second, preferred_element_type=jnp.float32) + b_second).astype(
        jnp.bfloat16
    )


def solution(mesh):
    return jax.shard_map(
        per_device,
        mesh=mesh,
        in_specs=(
            P("feat", "dom"),
            P("dom", None, None),
            P("dom", None),
            P(None, "dom"),
            P(None, "dom"),
            P("dom"),
            P(),
            P(),
            P(),
            P(),
            P(),
        ),
        out_specs=P(("dom", "feat"), None),
        check_vma=False,
    )
```

profile of v0, /device:TPU:0, one launch (start us, length us, event | category | flops | bytes accessed | tf_op | source)
XLA Modules:
  0.0 211.6 jit_solution(9336889372195347211)
XLA Ops:
  0.0 0.0 copy-start
  0.0 3.3 %copy.22 = bf16[128,8192]{0,1:T(8,128)(2,1)S(1)} copy(bf16[128,8192]{1,0:T(8,128)(2,1)} %param.13) | data formatting | bytes 4194304 | tf_op args[0]
  3.3 0.0 copy-done.4
  3.3 0.1 reshape.142
  3.4 0.0 copy-done.8
  3.4 0.1 iota_compare_fusion.2
  3.5 2.1 %gather_fusion.1 = bf16[64,128,128]{1,2,0:T(8,128)(2,1)} fusion(bf16[64,128,128]{1,2,0:T(8,128)(2,1)S(1)} %bitcast.68, s32[1024]{0:T(1024)S(1)} %pad_clamp_fusion.1), kind=kCustom, calls=%fused_computation.1 | custom fusion | bytes 4194560 | tf_op jit(solution)/shard_map/gather | solution.py:52
  5.6 3.1 %broadcast_select_fusion = bf16[8,8,128,128]{2,3,1,0:T(8,128)(2,1)} fusion(bf16[8,8,128,128]{2,3,1,0:T(8,128)(2,1)} %bitcast.70, pred[8,8]{1,0:T(8,128)(4,1)S(1)} %iota_compare_fusion.2), kind=kLoop, calls=%fused_computation.22 | loop fusion | flops 1048576 | bytes 4194368 | tf_op jit(solution)/shard_map/jit(_where)/select_n | solution.py:54
  8.8 5.2 %all-to-all-start = ((bf16[8,8,128,128]{2,3,1,0:T(8,128)(2,1)}), bf16[8,8,128,128]{2,3,1,0:T(8,128)(2,1)}, u32[]{:S(2)}, u32[]{:S(2)}) async-start(bf16[8,8,128,128]{2,3,1,0:T(8,128)(2,1)} %broadcast_select_fusion), calls=%async_computation | async-start | bytes 4194304 | tf_op jit(solution)/shard_map/all_to_all | solution.py:55
  14.0 1.3 copy.31
  15.2 0.0 copy-done.3
  15.2 0.1 copy.21
  16.0 0.0 copy-done.2
  16.0 0.8 fusion.16
  16.8 23.9 %all-to-all-done = bf16[8,8,128,128]{2,3,1,0:T(8,128)(2,1)} async-done(((bf16[8,8,128,128]{2,3,1,0:T(8,128)(2,1)}), bf16[8,8,128,128]{2,3,1,0:T(8,128)(2,1)}, u32[]{:S(2)}, u32[]{:S(2)}) %all-to-all-start) | async-done | bytes 2097184 | tf_op jit(solution)/shard_map/all_to_all | solution.py:55
  40.7 3.9 %pad_maximum_fusion = bf16[128,128,128]{1,2,0:T(8,128)(2,1)} fusion(bf16[64,128,128]{1,2,0:T(8,128)(2,1)} %bitcast.9, bf16[64,128,128]{1,2,0:T(8,128)(2,1)S(1)} %bitcast.69), kind=kLoop, calls=%fused_computation.19 | loop fusion | flops 2097152 | bytes 8388608 | tf_op jit(solution)/shard_map/concatenate | solution.py:59
  44.6 6.4 %copy.24 = bf16[128,128,128]{2,1,0:T(8,128)(2,1)} copy(bf16[128,128,128]{1,2,0:T(8,128)(2,1)} %pad_maximum_fusion) | data formatting | bytes 8388608
  50.9 94.6 %while.11 = (s32[]{:T(128)}, f32[4,16,128,128]{3,2,1,0:T(8,128)}, s32[4,24,16]{1,2,0:T(8,128)S(1)}, bf16[128,128,128]{2,1,0:T(8,128)(2,1)}, s32[4,24,16,128]{3,2...) while((s32[]{:T(128)}, f32[4,16,128,128]{3,2,1,0:T(8,128)}, ...), condition=%wide.region_1.2_spmd.clone, body=%wide.region_0.1_spmd.clone.sunk | while | flops 1623197824 | bytes 39702104 | solution.py:29
  50.9 0.1 copy.35
  51.0 0.1 reshape.160
  51.1 13.6 %gather_fusion = bf16[384,128,128]{2,1,0:T(8,128)(2,1)} fusion(bf16[128,128,128]{2,1,0:T(8,128)(2,1)} %get-tuple-element.135, s32[1024]{0:T(1024)S(1)} %pad_clamp_fusion.3), kind=kCustom, calls=%fused_computation.clone.clone.1 | custom fusion | bytes 25167360 | tf_op jit(solution)/shard_map/while/body/eval_jaxpr/gather | solution.py:21
  64.8 0.9 dynamic-slice_bitcast_fusion.5
  65.7 9.0 %fusion.27 = f32[4,16,128,128]{3,2,1,0:T(8,128)} fusion(f32[4,16,128,128]{3,2,1,0:T(8,128)} %get-tuple-element.126, s32[]{:T(128)} %get-tuple-element.125, bf16[24,16,128,128]{3,2,1,0:T(8,128)(2,1)} %bitcast.67, s32[24,16,128]{2,1,0:T(8,128)S(1)} %dynamic-slice_bitcast_fusion.4, bf16[24,16,128]{2,1,0:T(8,128)(2,1)S(1)} %dynamic-slice_bitcast_fusion.5), kind=kOutput, calls=%fused_computation.10.clone.1 | convolution fusion | flops 1623195648 | bytes 13926912 | tf_op jit(solution)/shard_map/while/body/eval_jaxpr/kgcs,kgsd->gcd/dot_general | solution.py:27
  74.7 0.1 copy.35
  74.8 0.1 reshape.160
  74.9 13.5 %gather_fusion = bf16[384,128,128]{2,1,0:T(8,128)(2,1)} fusion(bf16[128,128,128]{2,1,0:T(8,128)(2,1)} %get-tuple-element.135, s32[1024]{0:T(1024)S(1)} %pad_clamp_fusion.3), kind=kCustom, calls=%fused_computation.clone.clone.1 | custom fusion | bytes 25167360 | tf_op jit(solution)/shard_map/while/body/eval_jaxpr/gather | solution.py:21
  88.4 0.9 dynamic-slice_bitcast_fusion.5
  89.3 9.0 %fusion.27 = f32[4,16,128,128]{3,2,1,0:T(8,128)} fusion(f32[4,16,128,128]{3,2,1,0:T(8,128)} %get-tuple-element.126, s32[]{:T(128)} %get-tuple-element.125, bf16[24,16,128,128]{3,2,1,0:T(8,128)(2,1)} %bitcast.67, s32[24,16,128]{2,1,0:T(8,128)S(1)} %dynamic-slice_bitcast_fusion.4, bf16[24,16,128]{2,1,0:T(8,128)(2,1)S(1)} %dynamic-slice_bitcast_fusion.5), kind=kOutput, calls=%fused_computation.10.clone.1 | convolution fusion | flops 1623195648 | bytes 13926912 | tf_op jit(solution)/shard_map/while/body/eval_jaxpr/kgcs,kgsd->gcd/dot_general | solution.py:27
  98.3 0.1 copy.35
  98.4 0.1 reshape.160
  98.5 13.5 %gather_fusion = bf16[384,128,128]{2,1,0:T(8,128)(2,1)} fusion(bf16[128,128,128]{2,1,0:T(8,128)(2,1)} %get-tuple-element.135, s32[1024]{0:T(1024)S(1)} %pad_clamp_fusion.3), kind=kCustom, calls=%fused_computation.clone.clone.1 | custom fusion | bytes 25167360 | tf_op jit(solution)/shard_map/while/body/eval_jaxpr/gather | solution.py:21
  112.0 0.9 dynamic-slice_bitcast_fusion.5
  112.9 9.0 %fusion.27 = f32[4,16,128,128]{3,2,1,0:T(8,128)} fusion(f32[4,16,128,128]{3,2,1,0:T(8,128)} %get-tuple-element.126, s32[]{:T(128)} %get-tuple-element.125, bf16[24,16,128,128]{3,2,1,0:T(8,128)(2,1)} %bitcast.67, s32[24,16,128]{2,1,0:T(8,128)S(1)} %dynamic-slice_bitcast_fusion.4, bf16[24,16,128]{2,1,0:T(8,128)(2,1)S(1)} %dynamic-slice_bitcast_fusion.5), kind=kOutput, calls=%fused_computation.10.clone.1 | convolution fusion | flops 1623195648 | bytes 13926912 | tf_op jit(solution)/shard_map/while/body/eval_jaxpr/kgcs,kgsd->gcd/dot_general | solution.py:27
  121.9 0.1 copy.35
  122.0 0.1 reshape.160
  122.1 13.5 %gather_fusion = bf16[384,128,128]{2,1,0:T(8,128)(2,1)} fusion(bf16[128,128,128]{2,1,0:T(8,128)(2,1)} %get-tuple-element.135, s32[1024]{0:T(1024)S(1)} %pad_clamp_fusion.3), kind=kCustom, calls=%fused_computation.clone.clone.1 | custom fusion | bytes 25167360 | tf_op jit(solution)/shard_map/while/body/eval_jaxpr/gather | solution.py:21
  135.6 0.9 dynamic-slice_bitcast_fusion.5
  136.5 9.0 %fusion.27 = f32[4,16,128,128]{3,2,1,0:T(8,128)} fusion(f32[4,16,128,128]{3,2,1,0:T(8,128)} %get-tuple-element.126, s32[]{:T(128)} %get-tuple-element.125, bf16[24,16,128,128]{3,2,1,0:T(8,128)(2,1)} %bitcast.67, s32[24,16,128]{2,1,0:T(8,128)S(1)} %dynamic-slice_bitcast_fusion.4, bf16[24,16,128]{2,1,0:T(8,128)(2,1)S(1)} %dynamic-slice_bitcast_fusion.5), kind=kOutput, calls=%fused_computation.10.clone.1 | convolution fusion | flops 1623195648 | bytes 13926912 | tf_op jit(solution)/shard_map/while/body/eval_jaxpr/kgcs,kgsd->gcd/dot_general | solution.py:27
  145.6 0.0 copy-done.1
  145.6 4.0 %fusion.15 = bf16[128,8192]{1,0:T(8,128)(2,1)} fusion(f32[64,16,8,128]{3,2,1,0:T(8,128)} %bitcast.72, bf16[128,8192]{1,0:T(8,128)(2,1)S(1)} %copy-done.1, f32[]{:T(128)} %bitcast), kind=kLoop, calls=%fused_computation.18 | loop fusion | flops 4194304 | bytes 8388612 | tf_op jit(solution)/shard_map/convert_element_type | solution.py:62
  149.6 3.3 %reshape.130 = bf16[128,4,4,512]{3,2,1,0:T(4,128)(2,1)S(1)} reshape(bf16[128,8192]{1,0:T(8,128)(2,1)} %fusion.15) | data formatting | bytes 4194304 | tf_op jit(solution)/shard_map/reshape | solution.py:66
  152.9 0.7 copy.27
  153.7 0.0 copy-start.5
  153.7 0.0 copy-start.6
  153.7 0.0 copy-start.7
  153.7 50.6 %all_to_all.20 = bf16[128,4,4,512]{3,2,0,1:T(4,128)(2,1)S(1)} all-to-all(bf16[128,4,4,512]{3,2,0,1:T(4,128)(2,1)S(1)} %copy.27), channel_id=1, replica_groups=mesh['dom'=8,'feat'=4] {'feat'}, dimensions={1} | all-to-all | bytes 4194304 | tf_op jit(solution)/shard_map/all_to_all | solution.py:67
  204.3 2.0 copy.32
  206.3 5.3 %add_convert_fusion = bf16[2048,512]{1,0:T(8,128)(2,1)} fusion(bf16[512,512]{1,0:T(8,128)(2,1)S(1)} %copy-done, f32[512]{0:T(512)S(1)} %copy-done.6, bf16[512,2048]{1,0:T(8,128)(2,1)} %bitcast.74, bf16[512,512]{1,0:T(8,128)(2,1)S(1)} %copy-done.5, f32[512]{0:T(512)S(1)} %copy-done.7), kind=kOutput, calls=%fused_computation.20 | convolution fusion | flops 2152726528 | bytes 5246976 | tf_op jit(solution)/shard_map/dot_general | solution.py:76
  (28 shorter events, 0.2 us)
Async XLA Ops:
  0.0 206.2 %copy-start = (bf16[512,512]{1,0:T(8,128)(2,1)S(1)}, bf16[512,512]{1,0:T(8,128)(2,1)}, u32[]{:S(2)}) copy-start(bf16[512,512]{1,0:T(8,128)(2,1)} %param.22) | copy-start | bytes 1572868
  0.0 3.3 %copy-start.4 = (s32[1,8,8]{2,1,0:T(8,128)S(1)}, s32[1,8,8]{2,1,0:T(8,128)}, u32[]{:S(2)}) copy-start(s32[1,8,8]{2,1,0:T(8,128)} %param.14) | copy-start | bytes 772
  0.0 3.4 %copy-start.8 = (s32[1,8]{1,0:T(1,128)S(1)}, s32[1,8]{1,0:T(1,128)}, u32[]{:S(2)}) copy-start(s32[1,8]{1,0:T(1,128)} %param.15) | copy-start | bytes 100
  5.6 9.6 %copy-start.3 = (s32[24,64]{1,0:T(8,128)S(1)}, s32[24,64]{1,0:T(8,128)}, u32[]{:S(2)}) copy-start(s32[24,64]{1,0:T(8,128)} %param.16) | copy-start | bytes 18436
  5.6 10.4 %copy-start.2 = (s32[8192]{0:T(1024)S(1)}, s32[8192]{0:T(1024)}, u32[]{:S(2)}) copy-start(s32[8192]{0:T(1024)} %param.18) | copy-start | bytes 98308
  8.8 31.9 %all-to-all-start = ((bf16[8,8,128,128]{2,3,1,0:T(8,128)(2,1)}), bf16[8,8,128,128]{2,3,1,0:T(8,128)(2,1)}, u32[]{:S(2)}, u32[]{:S(2)}) async-start(bf16[8,8,128,128]{2,3,1,0:T(8,128)(2,1)} %broadcast_select_fusion), calls=%async_computation | async-start | bytes 4194304 | tf_op jit(solution)/shard_map/all_to_all | solution.py:55
  50.9 94.6 %copy-start.1 = (bf16[128,8192]{1,0:T(8,128)(2,1)S(1)}, bf16[128,8192]{1,0:T(8,128)(2,1)}, u32[]{:S(2)}) copy-start(bf16[128,8192]{1,0:T(8,128)(2,1)} %param.13) | copy-start | bytes 6291460
  153.7 52.6 %copy-start.5 = (bf16[512,512]{1,0:T(8,128)(2,1)S(1)}, bf16[512,512]{1,0:T(8,128)(2,1)}, u32[]{:S(2)}) copy-start(bf16[512,512]{1,0:T(8,128)(2,1)} %param.20) | copy-start | bytes 1572868
  153.7 52.6 %copy-start.6 = (f32[512]{0:T(512)S(1)}, f32[512]{0:T(512)}, u32[]{:S(2)}) copy-start(f32[512]{0:T(512)} %param.23) | copy-start | bytes 6148
  153.7 52.6 %copy-start.7 = (f32[512]{0:T(512)S(1)}, f32[512]{0:T(512)}, u32[]{:S(2)}) copy-start(f32[512]{0:T(512)} %param.21) | copy-start | bytes 6148
where the time goes:
time: 213 us; the launch traced here: 212 us
  local copies, waits for them, and re-layouts  77.7 us (36%)
  blocking collectives  50.6 us (24%)
  matrix products  41.4 us (19%)
  waiting for transfers between devices  23.9 us (11%)
  other arithmetic  12.1 us (6%)
  starting transfers between devices  5.21 us (2%)
    gather x4, local copies, waits for them, and re-layouts, one_step(): gathered = table[triple[0]]  54.2 us
    all_to_all x1, blocking collectives, per_device(): lax.all_to_all(shaped, 'feat', split_axis=1, concat_axis=0, tiled=True)  50.6 us
    dot_general x4, matrix products, one_step(): jnp.einsum('kgcs,kgsd->gcd', gathered, onehot, preferred_element_type=jnp...  36.1 us
    all_to_all x1, waiting for transfers between devices, per_device(): lax.all_to_all(chosen, 'dom', split_axis=0, concat_axis=0, tiled=True)  23.9 us
    unnamed x23, local copies, waits for them, and re-layouts  13 us
    dot_general x1, matrix products, per_device(): jnp.dot(activated, w_second, preferred_element_type=jnp.float32) + b_second  5.3 us
    all_to_all x1, starting transfers between devices, per_device(): lax.all_to_all(chosen, 'dom', split_axis=0, concat_axis=0, tiled=True)  5.21 us
  transfers between devices with their start and end apart: 1, of which 1 were waited for; matrix products, arithmetic and copies ran while one was open for 1% of the time, Pallas kernels for 0%

commit v1 on v0

v1 whole, which is shorter than its diff:
```python
import functools

import jax
import jax.numpy as jnp
from jax import lax
from jax.experimental import pallas as pl
from jax.experimental.pallas import tpu as pltpu
from jax.sharding import PartitionSpec as P

BLOCK = 128
CHUNKS = 4
NODE_TILE = 256


def kernel(
    parts, groups, chunks,
    sb_ref, cnt_ref, tile_ref, eps_ref,
    feat_ref, nbr_ref, deg_ref, w1_ref, b1_ref, w2_ref, b2_ref,
    out_ref,
    *scratch,
):
    tables = scratch[:chunks]
    local, stage, zstage, parcel, hsend, hrecv, zsend, zrecv = scratch[chunks:]
    me = lax.axis_index("dom")
    z = lax.axis_index("feat")
    slots = stage.shape[2]
    width = tables[0].shape[1]
    list_width, block_count = tile_ref.shape
    per_group = block_count // groups
    half = groups // 2

    def lanes(block):
        return pl.ds(pl.multiple_of(block * BLOCK, BLOCK), BLOCK)

    def halo_copy(c, peer, source):
        return pltpu.make_async_remote_copy(
            src_ref=stage.at[c, peer],
            dst_ref=tables[c].at[pl.ds(block_count + source * slots, slots)],
            send_sem=hsend.at[c, peer],
            recv_sem=hrecv.at[c, source],
            device_id={"dom": peer},
            device_id_type=pl.DeviceIdType.MESH,
        )

    def row_copy(c, dest, source):
        return pltpu.make_async_remote_copy(
            src_ref=zstage.at[c, dest],
            dst_ref=parcel.at[source, c],
            send_sem=zsend.at[c, dest],
            recv_sem=zrecv.at[c, source],
            device_id={"feat": dest},
            device_id_type=pl.DeviceIdType.MESH,
        )

    def dest_of(k):
        if k < half:
            return lax.rem(z // half + 1, 2) * half + lax.rem(lax.rem(z, half) + k, half)
        return (z // half) * half + lax.rem(lax.rem(z, half) + (k - half + 1), half)

    @pl.loop(0, block_count)
    def _(b):
        for c in range(chunks):
            block = feat_ref[pl.ds(c * width, width), lanes(b)]
            local[b, c] = block
            tables[c][b] = block

    barrier = pltpu.get_barrier_semaphore()

    @pl.loop(1, parts)
    def _(k):
        pl.semaphore_signal(
            barrier, inc=1, device_id={"dom": lax.rem(me + k, parts)},
            device_id_type=pl.DeviceIdType.MESH,
        )

    @pl.loop(1, groups)
    def _(k):
        pl.semaphore_signal(
            barrier, inc=1, device_id={"feat": lax.rem(z + k, groups)},
            device_id_type=pl.DeviceIdType.MESH,
        )

    pl.semaphore_wait(barrier, parts + groups - 2)

    for c in range(chunks):
        @pl.loop(1, parts)
        def _(k):
            peer = lax.rem(me + k, parts)
            for s in range(slots):
                used = (s < cnt_ref[0, peer]).astype(jnp.float32)
                block = local[sb_ref[0, peer, s], c]
                stage[c, peer, s] = (block.astype(jnp.float32) * used).astype(jnp.bfloat16)
            halo_copy(c, peer, me).start()

    for c in range(chunks):
        tables[c][pl.ds(block_count + me * slots, slots)] = jnp.zeros(
            (slots, width, BLOCK), jnp.bfloat16
        )

    gain = 1.0 + eps_ref[0]

    def mixed_block(c, b):
        total = gain * feat_ref[pl.ds(c * width, width), lanes(b)].astype(jnp.float32)
        near = jnp.zeros((width, BLOCK), jnp.float32)
        degree = deg_ref[pl.ds(b, 1), :]
        for j in range(list_width):
            tile = tables[c][tile_ref[j, b]].astype(jnp.float32)
            index = jnp.broadcast_to(nbr_ref[pl.ds(j, 1), lanes(b)], (width, BLOCK))
            taken = jnp.take_along_axis(tile, index, axis=1, mode="promise_in_bounds")
            live = jnp.broadcast_to(degree, (width, BLOCK)) > j
            near = near + jnp.where(live, taken, 0.0)
        return (total + near).astype(jnp.bfloat16)

    for c in range(chunks):
        @pl.loop(1, parts)
        def _(k):
            source = lax.rem(me + k, parts)
            halo_copy(c, source, source).wait_recv()

        for k in range(groups):
            dest = dest_of(k) if k < groups - 1 else z

            @pl.loop(0, per_group)
            def _(i):
                block = mixed_block(c, dest * per_group + i)
                if k < groups - 1:
                    zstage[c, dest, :, lanes(i)] = block
                else:
                    parcel[z, c, :, lanes(i)] = block

            if k < groups - 1:
                row_copy(c, dest, z).start()

    for c in range(chunks):
        @pl.loop(1, groups)
        def _(k):
            source = lax.rem(z + k, groups)
            row_copy(c, source, source).wait_recv()

    depth = w1_ref.shape[0]

    @pl.loop(0, out_ref.shape[0] // NODE_TILE)
    def _(n):
        nodes = pl.ds(pl.multiple_of(n * NODE_TILE, NODE_TILE), NODE_TILE)
        columns = parcel[:, :, :, nodes].reshape(depth, NODE_TILE)
        hidden = lax.dot_general(
            columns, w1_ref[...], (((0,), (0,)), ((), ())), preferred_element_type=jnp.float32
        ) + b1_ref[...]
        hidden = jnp.maximum(hidden, 0.0).astype(jnp.bfloat16)
        out_ref[nodes, :] = (
            jnp.dot(hidden, w2_ref[...], preferred_element_type=jnp.float32) + b2_ref[...]
        ).astype(jnp.bfloat16)

    for c in range(chunks):
        @pl.loop(1, parts)
        def _(k):
            halo_copy(c, lax.rem(me + k, parts), me).wait_send()

        @pl.loop(1, groups)
        def _(k):
            row_copy(c, lax.rem(z + k, groups), z).wait_send()


def per_device(
    features, send_blocks, counts, tile_blocks, neighbours, degree, epsilon,
    w_first, b_first, w_second, b_second,
):
    parts = lax.axis_size("dom")
    groups = lax.axis_size("feat")
    cols, rows = features.shape
    slots = send_blocks.shape[2]
    chunks = CHUNKS
    width = cols // chunks
    block_count = rows // BLOCK
    owned = rows // groups
    out_cols = w_second.shape[1]
    vmem = pl.BlockSpec(memory_space=pltpu.VMEM)
    smem = pl.BlockSpec(memory_space=pltpu.SMEM)
    return pl.pallas_call(
        functools.partial(kernel, parts, groups, chunks),
        out_shape=jax.ShapeDtypeStruct((owned, out_cols), jnp.bfloat16),
        in_specs=[smem] * 4 + [vmem] * 7,
        out_specs=vmem,
        scratch_shapes=[
            pltpu.VMEM((block_count + parts * slots, width, BLOCK), jnp.bfloat16)
            for _ in range(chunks)
        ] + [
            pltpu.VMEM((block_count, chunks, width, BLOCK), jnp.bfloat16),
            pltpu.VMEM((chunks, parts, slots, width, BLOCK), jnp.bfloat16),
            pltpu.VMEM((chunks, groups, width, owned), jnp.bfloat16),
            pltpu.VMEM((groups, chunks, width, owned), jnp.bfloat16),
            pltpu.SemaphoreType.DMA((chunks, parts)),
            pltpu.SemaphoreType.DMA((chunks, parts)),
            pltpu.SemaphoreType.DMA((chunks, groups)),
            pltpu.SemaphoreType.DMA((chunks, groups)),
        ],
        compiler_params=pltpu.CompilerParams(
            collective_id=0, has_side_effects=True, vmem_limit_bytes=56 * 1024 * 1024
        ),
    )(
        send_blocks, counts, tile_blocks, epsilon,
        features, neighbours, degree.reshape(block_count, BLOCK),
        w_first, b_first.reshape(1, -1), w_second, b_second.reshape(1, -1),
    )


def solution(mesh):
    return jax.shard_map(
        per_device,
        mesh=mesh,
        in_specs=(
            P("feat", "dom"),
            P("dom", None, None),
            P("dom", None),
            P(None, "dom"),
            P(None, "dom"),
            P("dom"),
            P(), P(), P(), P(), P(),
        ),
        out_specs=P(("dom", "feat"), None),
        check_vma=False,
    )
```

time: 213 us -> 79.4 us (0.37)
  Pallas kernels: 0 us -> 75.5 us
  local copies, waits for them, and re-layouts: 77.7 us -> 3.05 us
  blocking collectives: 50.6 us -> 0 us
  matrix products: 41.4 us -> 0 us
  waiting for transfers between devices: 23.9 us -> 0 us
  other arithmetic: 12.1 us -> 0 us
  starting transfers between devices: 5.21 us -> 0 us
    pallas_call x0 -> x1, Pallas kernels: none -> 75.5 us  [per_device(): pl.pallas_call(functools.partial(kernel, parts, groups, chunks), out_shap...]
    gather x5 -> x0, local copies, waits for them, and re-layouts: 56.3 us -> none  [the longest x4 54.2 us: one_step(): gathered = table[triple[0]]]
    all_to_all x1 -> x0, blocking collectives: 50.6 us -> none  [per_device(): lax.all_to_all(shaped, 'feat', split_axis=1, concat_axis=0, tiled=True)]
    dot_general x5 -> x0, matrix products: 41.4 us -> none  [the longest x4 36.1 us: one_step(): jnp.einsum('kgcs,kgsd->gcd', gathered, onehot, preferred_element_type=jnp...]
    all_to_all x1 -> x0, waiting for transfers between devices: 23.9 us -> none  [per_device(): lax.all_to_all(chosen, 'dom', split_axis=0, concat_axis=0, tiled=True)]
    unnamed x23 -> x1, local copies, waits for them, and re-layouts: 13 us -> 3.05 us
    all_to_all x1 -> x0, starting transfers between devices: 5.21 us -> none  [per_device(): lax.all_to_all(chosen, 'dom', split_axis=0, concat_axis=0, tiled=True)]
    convert_element_type x2 -> x0, other arithmetic: 4.87 us -> none  [the longest x1 4.03 us: per_device(): ((1.0 + epsilon[0]) * features.astype(jnp.float32) + near_sum).astype(jnp...]
  transfers between devices with their start and end apart: 1 -> 0, of which waited for: 1 -> 0; matrix products, arithmetic and copies ran while one was open for 1% -> 0% of each run, Pallas kernels for 0% -> 0%
where the time goes in v1:
time: 79.4 us; the launch traced here: 79.2 us
  Pallas kernels  75.5 us (95%)
  local copies, waits for them, and re-layouts  3.05 us (4%)
    pallas_call x1, Pallas kernels, per_device(): pl.pallas_call(functools.partial(kernel, parts, groups, chunks), out_shap...  75.5 us
    unnamed x1, local copies, waits for them, and re-layouts  3.05 us

profile of v1, /device:TPU:0, one launch (start us, length us, event | category | flops | bytes accessed | tf_op | source)
XLA Modules:
  0.0 79.2 jit_solution(8837201474971176335)
XLA Ops:
  0.7 75.5 %shard_map.109 = bf16[2048,512]{1,0:T(8,128)(2,1)} custom-call(s32[1,8,8]{2,1,0:T(8,128)} %sb_ref.1, s32[1,8]{1,0:T(1,128)} %cnt_ref.1, s32[24,64]{1,0:T(8,128)} %tile_ref.1, f32[1]{0:T(128)S(6)} %copy.13.eps_ref, bf16[128,8192]{1,0:T(8,128)(2,1)} %feat_ref.1, s32[24,8192]{1,0:T(8,128)} %nbr_ref.1, s32[64,128]{1,0:T(8,128)} %bitcast.3, ...), custom_call_target="tpu_custom_call" | custom-call | tf_op jit(solution)/shard_map/pallas_call | solution.py:179
  76.2 3.0 %copy.14 = bf16[2048,512]{1,0:T(8,128)(2,1)} copy(bf16[2048,512]{1,0:T(8,128)(2,1)} %shard_map.109) | data formatting | bytes 4194304

commit v2 on v1

v2 whole, which is shorter than its diff:
```python
import functools

import jax
import jax.numpy as jnp
from jax import lax
from jax.experimental import pallas as pl
from jax.experimental.pallas import tpu as pltpu
from jax.sharding import PartitionSpec as P

BLOCK = 128
SUBLANES = 16
PIECES = 4


def chunk_widths(cols):
    widths = []
    while sum(widths) < cols:
        widths.append(min(max(SUBLANES, sum(widths)), cols - sum(widths)))
    return widths


def kernel(
    parts, groups, pieces, widths,
    sb_ref, cnt_ref, tile_ref, eps_ref, deg_ref, b1_ref, b2_ref,
    feat_hbm, nbr_hbm, w1_hbm, w2_hbm,
    out_hbm,
    *scratch,
):
    chunks = len(widths)
    starts = [sum(widths[:c]) for c in range(chunks)]
    tables, locals_, stages, feats = (scratch[i * chunks:(i + 1) * chunks] for i in range(4))
    (nbr_ref, w1_ref, w2_ref, out_ref, zstage, parcel,
     hsend, hrecv, zsend, zrecv, in_sem, out_sem) = scratch[4 * chunks:]
    me = lax.axis_index("dom")
    z = lax.axis_index("feat")
    slots = stages[0].shape[1]
    list_width, block_count = tile_ref.shape
    per_piece = block_count // groups // pieces
    piece_nodes = per_piece * BLOCK
    half = groups // 2

    def lanes(block):
        return pl.ds(pl.multiple_of(block * BLOCK, BLOCK), BLOCK)

    def halo_copy(c, peer, source):
        return pltpu.make_async_remote_copy(
            src_ref=stages[c].at[peer],
            dst_ref=tables[c].at[pl.ds(block_count + source * slots, slots)],
            send_sem=hsend.at[c, peer],
            recv_sem=hrecv.at[c, source],
            device_id={"dom": peer},
            device_id_type=pl.DeviceIdType.MESH,
        )

    def row_copy(c, p, dest, source):
        span = pl.ds(starts[c], widths[c])
        return pltpu.make_async_remote_copy(
            src_ref=zstage.at[p, dest, span],
            dst_ref=parcel.at[p, source, span],
            send_sem=zsend.at[c, p, dest],
            recv_sem=zrecv.at[c, p, source],
            device_id={"feat": dest},
            device_id_type=pl.DeviceIdType.MESH,
        )

    def dest_of(k):
        if k < half:
            return lax.rem(z // half + 1, 2) * half + lax.rem(lax.rem(z, half) + k, half)
        return (z // half) * half + lax.rem(lax.rem(z, half) + (k - half + 1), half)

    barrier = pltpu.get_barrier_semaphore()

    @pl.loop(1, parts)
    def _(k):
        pl.semaphore_signal(
            barrier, inc=1, device_id={"dom": lax.rem(me + k, parts)},
            device_id_type=pl.DeviceIdType.MESH,
        )

    @pl.loop(1, groups)
    def _(k):
        pl.semaphore_signal(
            barrier, inc=1, device_id={"feat": lax.rem(z + k, groups)},
            device_id_type=pl.DeviceIdType.MESH,
        )

    loads = [
        pltpu.make_async_copy(
            feat_hbm.at[pl.ds(starts[c], widths[c])], feats[c], in_sem.at[c]
        )
        for c in range(chunks)
    ]
    loads.append(pltpu.make_async_copy(nbr_hbm, nbr_ref, in_sem.at[chunks]))
    loads.append(pltpu.make_async_copy(w1_hbm, w1_ref, in_sem.at[chunks + 1]))
    loads.append(pltpu.make_async_copy(w2_hbm, w2_ref, in_sem.at[chunks + 2]))
    for load in loads:
        load.start()

    for c in range(chunks):
        loads[c].wait()

        @pl.loop(0, block_count, unroll=4)
        def _(b):
            block = feats[c][:, lanes(b)]
            locals_[c][b] = block
            tables[c][b] = block

        if c == 0:
            pl.semaphore_wait(barrier, parts + groups - 2)

        @pl.loop(1, parts)
        def _(k):
            peer = lax.rem(me + k, parts)
            for s in range(slots):
                used = (s < cnt_ref[0, peer]).astype(jnp.float32)
                block = locals_[c][sb_ref[0, peer, s]]
                stages[c][peer, s] = (block.astype(jnp.float32) * used).astype(jnp.bfloat16)
            halo_copy(c, peer, me).start()

    for c in range(chunks):
        tables[c][pl.ds(block_count + me * slots, slots)] = jnp.zeros(
            (slots, widths[c], BLOCK), jnp.bfloat16
        )

    gain = 1.0 + eps_ref[0]
    loads[chunks].wait()

    def mixed_block(c, b):
        shape = (widths[c], BLOCK)
        total = gain * feats[c][:, lanes(b)].astype(jnp.float32)
        near = jnp.zeros(shape, jnp.float32)
        degree = jnp.broadcast_to(deg_ref[pl.ds(b, 1), :], shape)
        for j in range(list_width):
            tile = tables[c][tile_ref[j, b]].astype(jnp.float32)
            index = jnp.broadcast_to(nbr_ref[pl.ds(j, 1), lanes(b)], shape)
            taken = jnp.take_along_axis(tile, index, axis=1, mode="promise_in_bounds")
            near = near + jnp.where(degree > j, taken, 0.0)
        return (total + near).astype(jnp.bfloat16)

    for c in range(chunks):
        @pl.loop(1, parts)
        def _(k):
            source = lax.rem(me + k, parts)
            halo_copy(c, source, source).wait_recv()

        span = pl.ds(starts[c], widths[c])
        unroll = per_piece if widths[c] <= 2 * SUBLANES else max(per_piece // 2, 1)

        @pl.loop(0, pieces)
        def _(p):
            for k in range(groups):
                dest = dest_of(k) if k < groups - 1 else z
                first = (dest * pieces + p) * per_piece

                @pl.loop(0, per_piece, unroll=unroll)
                def _(i):
                    block = mixed_block(c, first + i)
                    if k < groups - 1:
                        zstage[p, dest, span, lanes(i)] = block
                    else:
                        parcel[p, z, span, lanes(i)] = block

                if k < groups - 1:
                    row_copy(c, p, dest, z).start()

    loads[chunks + 1].wait()
    loads[chunks + 2].wait()
    depth = w1_ref.shape[0]

    def out_copy(p):
        rows = pl.ds(pl.multiple_of(p * piece_nodes, piece_nodes), piece_nodes)
        return pltpu.make_async_copy(out_ref.at[rows], out_hbm.at[rows], out_sem.at[p])

    @pl.loop(0, pieces)
    def _(p):
        for c in range(chunks):
            @pl.loop(1, groups)
            def _(k):
                source = lax.rem(z + k, groups)
                row_copy(c, p, source, source).wait_recv()

        columns = parcel[p].reshape(depth, piece_nodes)
        hidden = lax.dot_general(
            columns, w1_ref[...], (((0,), (0,)), ((), ())), preferred_element_type=jnp.float32
        ) + b1_ref[...]
        hidden = jnp.maximum(hidden, 0.0).astype(jnp.bfloat16)
        rows = pl.ds(pl.multiple_of(p * piece_nodes, piece_nodes), piece_nodes)
        out_ref[rows, :] = (
            jnp.dot(hidden, w2_ref[...], preferred_element_type=jnp.float32) + b2_ref[...]
        ).astype(jnp.bfloat16)
        out_copy(p).start()

    for c in range(chunks):
        @pl.loop(1, parts)
        def _(k):
            halo_copy(c, lax.rem(me + k, parts), me).wait_send()

        @pl.loop(0, pieces)
        def _(p):
            @pl.loop(1, groups)
            def _(k):
                row_copy(c, p, lax.rem(z + k, groups), z).wait_send()

    @pl.loop(0, pieces)
    def _(p):
        out_copy(p).wait()


def per_device(
    features, send_blocks, counts, tile_blocks, neighbours, degree, epsilon,
    w_first, b_first, w_second, b_second,
):
    parts = lax.axis_size("dom")
    groups = lax.axis_size("feat")
    cols, rows = features.shape
    slots = send_blocks.shape[2]
    widths = chunk_widths(cols)
    chunks = len(widths)
    block_count = rows // BLOCK
    owned = rows // groups
    pieces = min(PIECES, owned // BLOCK)
    hidden_cols, out_cols = w_second.shape
    depth = w_first.shape[0]
    vmem = pl.BlockSpec(memory_space=pltpu.VMEM)
    smem = pl.BlockSpec(memory_space=pltpu.SMEM)
    anywhere = pl.BlockSpec(memory_space=pl.ANY)
    bf16 = jnp.bfloat16
    return pl.pallas_call(
        functools.partial(kernel, parts, groups, pieces, widths),
        out_shape=jax.ShapeDtypeStruct((owned, out_cols), bf16),
        in_specs=[smem] * 4 + [vmem] * 3 + [anywhere] * 4,
        out_specs=anywhere,
        scratch_shapes=[
            pltpu.VMEM((block_count + parts * slots, w, BLOCK), bf16) for w in widths
        ] + [
            pltpu.VMEM((block_count, w, BLOCK), bf16) for w in widths
        ] + [
            pltpu.VMEM((parts, slots, w, BLOCK), bf16) for w in widths
        ] + [
            pltpu.VMEM((w, rows), bf16) for w in widths
        ] + [
            pltpu.VMEM(neighbours.shape, jnp.int32),
            pltpu.VMEM((depth, hidden_cols), bf16),
            pltpu.VMEM((hidden_cols, out_cols), bf16),
            pltpu.VMEM((owned, out_cols), bf16),
            pltpu.VMEM((pieces, groups, cols, owned // pieces), bf16),
            pltpu.VMEM((pieces, groups, cols, owned // pieces), bf16),
            pltpu.SemaphoreType.DMA((chunks, parts)),
            pltpu.SemaphoreType.DMA((chunks, parts)),
            pltpu.SemaphoreType.DMA((chunks, pieces, groups)),
            pltpu.SemaphoreType.DMA((chunks, pieces, groups)),
            pltpu.SemaphoreType.DMA((chunks + 3,)),
            pltpu.SemaphoreType.DMA((pieces,)),
        ],
        compiler_params=pltpu.CompilerParams(
            collective_id=0, has_side_effects=True, vmem_limit_bytes=56 * 1024 * 1024
        ),
    )(
        send_blocks, counts, tile_blocks, epsilon,
        degree.reshape(block_count, BLOCK), b_first.reshape(1, -1), b_second.reshape(1, -1),
        features, neighbours, w_first, w_second,
    )


def solution(mesh):
    return jax.shard_map(
        per_device,
        mesh=mesh,
        in_specs=(
            P("feat", "dom"),
            P("dom", None, None),
            P("dom", None),
            P(None, "dom"),
            P(None, "dom"),
            P("dom"),
            P(), P(), P(), P(), P(),
        ),
        out_specs=P(("dom", "feat"), None),
        check_vma=False,
    )
```

time: 79.4 us -> 65.5 us (0.82)
  Pallas kernels: 75.5 us -> 61.6 us
    pallas_call x1, Pallas kernels: 75.5 us -> 61.6 us  [per_device(): pl.pallas_call(functools.partial(kernel, parts, groups, pieces, widths),...]
where the time goes in v2:
time: 65.5 us; the launch traced here: 65.3 us
  Pallas kernels  61.6 us (94%)
  local copies, waits for them, and re-layouts  3.05 us (5%)
  between operations  0.66 us (1%)
    pallas_call x1, Pallas kernels, per_device(): pl.pallas_call(functools.partial(kernel, parts, groups, pieces, widths),...  61.6 us
    unnamed x1, local copies, waits for them, and re-layouts  3.05 us

profile of v2, /device:TPU:0, one launch (start us, length us, event | category | flops | bytes accessed | tf_op | source)
XLA Modules:
  0.0 65.3 jit_solution(2257932065609628134)
XLA Ops:
  0.7 61.6 %shard_map.109 = bf16[2048,512]{1,0:T(8,128)(2,1)} custom-call(s32[1,8,8]{2,1,0:T(8,128)} %sb_ref.1, s32[1,8]{1,0:T(1,128)} %cnt_ref.1, s32[24,64]{1,0:T(8,128)} %tile_ref.1, f32[1]{0:T(128)S(6)} %copy.13.eps_ref, s32[64,128]{1,0:T(8,128)} %bitcast.3, f32[1,512]{1,0:T(1,128)} %bitcast.4, f32[1,512]{1,0:T(1,128)} %bitcast.5, bf16[128,8192]{1,0:T(8,128)(2,1)} %feat_hbm.1, ...), custom_call_target="tpu_custom_call" | custom-call | tf_op jit(solution)/shard_map/pallas_call | solution.py:228
  62.3 3.0 %copy.14 = bf16[2048,512]{1,0:T(8,128)(2,1)} copy(bf16[2048,512]{1,0:T(8,128)(2,1)} %shard_map.109) | data formatting | bytes 4194304

commit v3 on v2

--- a/solution.py
+++ b/solution.py
@@ -23,14 +23,14 @@
     parts, groups, pieces, widths,
     sb_ref, cnt_ref, tile_ref, eps_ref, deg_ref, b1_ref, b2_ref,
     feat_hbm, nbr_hbm, w1_hbm, w2_hbm,
-    out_hbm,
+    out_ref,
     *scratch,
 ):
     chunks = len(widths)
     starts = [sum(widths[:c]) for c in range(chunks)]
     tables, locals_, stages, feats = (scratch[i * chunks:(i + 1) * chunks] for i in range(4))
-    (nbr_ref, w1_ref, w2_ref, out_ref, zstage, parcel,
-     hsend, hrecv, zsend, zrecv, in_sem, out_sem) = scratch[4 * chunks:]
+    (nbr_ref, w1_ref, w2_ref, zstage, parcel,
+     hsend, hrecv, zsend, zrecv, in_sem) = scratch[4 * chunks:]
     me = lax.axis_index("dom")
     z = lax.axis_index("feat")
     slots = stages[0].shape[1]
@@ -167,10 +167,6 @@
     loads[chunks + 2].wait()
     depth = w1_ref.shape[0]
 
-    def out_copy(p):
-        rows = pl.ds(pl.multiple_of(p * piece_nodes, piece_nodes), piece_nodes)
-        return pltpu.make_async_copy(out_ref.at[rows], out_hbm.at[rows], out_sem.at[p])
-
     @pl.loop(0, pieces)
     def _(p):
         for c in range(chunks):
@@ -188,7 +184,6 @@
         out_ref[rows, :] = (
             jnp.dot(hidden, w2_ref[...], preferred_element_type=jnp.float32) + b2_ref[...]
         ).astype(jnp.bfloat16)
-        out_copy(p).start()
 
     for c in range(chunks):
         @pl.loop(1, parts)
@@ -200,10 +195,6 @@
             @pl.loop(1, groups)
             def _(k):
                 row_copy(c, p, lax.rem(z + k, groups), z).wait_send()
-
-    @pl.loop(0, pieces)
-    def _(p):
-        out_copy(p).wait()
 
 
 def per_device(
@@ -227,9 +218,9 @@
     bf16 = jnp.bfloat16
     return pl.pallas_call(
         functools.partial(kernel, parts, groups, pieces, widths),
-        out_shape=jax.ShapeDtypeStruct((owned, out_cols), bf16),
+        out_shape=pltpu.VMEM((owned, out_cols), bf16),
         in_specs=[smem] * 4 + [vmem] * 3 + [anywhere] * 4,
-        out_specs=anywhere,
+        out_specs=vmem,
         scratch_shapes=[
             pltpu.VMEM((block_count + parts * slots, w, BLOCK), bf16) for w in widths
         ] + [
@@ -242,7 +233,6 @@
             pltpu.VMEM(neighbours.shape, jnp.int32),
             pltpu.VMEM((depth, hidden_cols), bf16),
             pltpu.VMEM((hidden_cols, out_cols), bf16),
-            pltpu.VMEM((owned, out_cols), bf16),
             pltpu.VMEM((pieces, groups, cols, owned // pieces), bf16),
             pltpu.VMEM((pieces, groups, cols, owned // pieces), bf16),
             pltpu.SemaphoreType.DMA((chunks, parts)),
@@ -250,7 +240,6 @@
             pltpu.SemaphoreType.DMA((chunks, pieces, groups)),
             pltpu.SemaphoreType.DMA((chunks, pieces, groups)),
             pltpu.SemaphoreType.DMA((chunks + 3,)),
-            pltpu.SemaphoreType.DMA((pieces,)),
         ],
         compiler_params=pltpu.CompilerParams(
             collective_id=0, has_side_effects=True, vmem_limit_bytes=56 * 1024 * 1024

time: 65.5 us -> 63.7 us (0.973)
  local copies, waits for them, and re-layouts: 3.05 us -> 1.32 us
    unnamed x1, local copies, waits for them, and re-layouts: 3.05 us -> 1.32 us
where the time goes in v3:
time: 63.7 us; the launch traced here: 63.5 us
  Pallas kernels  61.5 us (97%)
  local copies, waits for them, and re-layouts  1.32 us (2%)
  between operations  0.66 us (1%)
    pallas_call x1, Pallas kernels, per_device(): pl.pallas_call(functools.partial(kernel, parts, groups, pieces, widths),...  61.5 us
    unnamed x1, local copies, waits for them, and re-layouts  1.32 us

profile of v3, /device:TPU:0, one launch (start us, length us, event | category | flops | bytes accessed | tf_op | source)
XLA Modules:
  0.0 63.5 jit_solution(15372686443954258179)
XLA Ops:
  0.7 61.5 %shard_map.109 = bf16[2048,512]{1,0:T(8,128)(2,1)S(1)} custom-call(s32[1,8,8]{2,1,0:T(8,128)} %sb_ref.1, s32[1,8]{1,0:T(1,128)} %cnt_ref.1, s32[24,64]{1,0:T(8,128)} %tile_ref.1, f32[1]{0:T(128)S(6)} %copy.14.eps_ref, s32[64,128]{1,0:T(8,128)} %bitcast.3, f32[1,512]{1,0:T(1,128)} %bitcast.4, f32[1,512]{1,0:T(1,128)} %bitcast.5, bf16[128,8192]{1,0:T(8,128)(2,1)} %feat_hbm.1, ...), custom_call_target="tpu_custom_call" | custom-call | tf_op jit(solution)/shard_map/pallas_call | solution.py:219
  62.2 1.3 %copy.13 = bf16[2048,512]{1,0:T(8,128)(2,1)} copy(bf16[2048,512]{1,0:T(8,128)(2,1)S(1)} %shard_map.109) | data formatting | bytes 4194304
